TPU v7x, 256 devices: a 4x2x16 block of a 4x16x16 slice. The times are simulated.
256 devices in a mesh: groups: 2 (over y), blk: 128 (over z, x, core).
Axes of the slice: x: 4, y: 2, z: 16, core: 2. Of those that a mesh axis runs over, the one named last changes fastest.
The devices are a block of a 4x16x16 slice.
Arguments:
- basis: float32 [8, 512, 480, 128], P(None, ('groups', 'blk')), parts along dimension 1
- nbr_block: int32 [512, 14], P(('groups', 'blk')), parts along dimension 0, may hold values from 0 to 255, as said below
- nbr_type: int32 [512, 14], P(('groups', 'blk')), parts along dimension 0, may hold values from 0 to 7
- nbr_count: int32 [512], P(('groups', 'blk')), parts along dimension 0, may hold values from 2 to 14, as said below
- sphere_type: int32 [512, 128], P(('groups', 'blk')), parts along dimension 0, may hold values from 0 to 3
- trans: float32 [8, 480, 480], replicated, may hold values from -0.25 to 0.25
- coup: float32 [8, 128, 128], replicated, may hold values from -0.5 to 0.5
- tmat: float32 [4, 480, 480], replicated, may hold values from -0.125 to 0.125
Outputs:
- new_vectors: float32 [2, 512, 480, 128], P(None, ('groups', 'blk')), parts along dimension 1
- hess_first: float32 [18], P('groups'), parts along dimension 0
- hess_second: float32 [20], P('groups'), parts along dimension 0
There are 2 independent parts, one for each index of `groups`. A program takes and returns all parts, laid end to end along the dimension named above; an argument that names none is the same for every part. Nothing has to cross between parts.
Inputs may be any that keep to these rules, and one draw needn't show every extreme that they name: `nbr_block`: each entry lies within 2 blocks of its own block; a block may be near itself. The first two slots of block b hold, in either order, the blocks b - 2 and b + 2, clipped to the cluster. Block b uses the first nbr_count[b] slots of its lists; some run of blocks uses all 14.
All inputs are finite; a program needn't handle non-finite values.
Results may differ from a plain program's by a relative error of at most 0.0003.
Values sent between devices are 32-bit elements; how exact they have to be, the bound alone decides.
A program may use at most 128 MiB of HBM per device.

v0:
```python
import functools

import jax
import jax.numpy as jnp
import numpy as np
from jax import lax
from jax.experimental import pallas as pl
from jax.experimental.pallas import tpu as pltpu
from jax.sharding import PartitionSpec as P

GB = ("groups", "blk")
PLANE = 8
LANES = 128
F32 = jnp.float32
BF16 = jnp.bfloat16
MESH = pl.DeviceIdType.MESH


def chunk_rows(coef):
    return [(c, min(LANES, coef - c)) for c in range(0, coef, LANES)]


def lane_tables(most):
    one = most
    table = np.zeros((8, LANES), np.int32)
    table[0:2, :] = most + 1
    lane_of = {}
    for i in range(most):
        table[0:3, i] = (i, one, -2)
    table[0:3, most] = (one, one, 1)
    at = most + 1
    for i in range(most):
        for j in range(i, most):
            table[0:3, at] = (i, j, 1 if i == j else 2)
            lane_of[i, j] = at
            at += 1
    return table, lane_of, at


def halves(x):
    high = x.astype(BF16)
    return high, (x - high.astype(F32)).astype(BF16)


def kernel(
    n_blk,
    cells,
    lane_of,
    basis_hbm,
    nbr_block,
    nbr_type,
    nbr_count,
    sphere_type,
    table,
    trans_hbm,
    coup_hbm,
    tmat_hbm,
    new_hbm,
    hess_ref,
    wins,
    stack,
    tr32,
    tm32,
    cp32,
    tr3,
    tm3,
    cp2,
    mix3,
    sum3,
    acc,
    image,
    rows_ref,
    plane_buf,
    ring_buf,
    weights,
    tr_sem,
    in_sem,
    out_sem,
    halo_send,
    halo_recv,
    plane_send,
    plane_recv,
    ring_send,
    ring_recv,
):
    n_vec, n_loc, coef, sph = basis_hbm.shape
    kinds = trans_hbm.shape[0]
    s_kinds = tmat_hbm.shape[0]
    slots = nbr_block.shape[1]
    most = n_vec + 1
    chunks = chunk_rows(coef)
    n_ring = n_blk // PLANE
    window = 3 * n_loc

    me = lax.axis_index("blk")
    z = me // PLANE
    q = me % PLANE
    left, right = me - 1, me + 1
    has_left, has_right = me > 0, me < n_blk - 1
    far_left = jnp.logical_and(q == 0, has_left)
    far_right = jnp.logical_and(q == PLANE - 1, has_right)

    own = pltpu.make_async_copy(
        basis_hbm.at[n_vec - 1], wins.at[0, pl.ds(n_loc, n_loc)], in_sem.at[0]
    )
    own.start()
    cp_copy = pltpu.make_async_copy(coup_hbm, cp32, in_sem.at[1])
    cp_copy.start()
    for t in range(kinds):
        pltpu.make_async_copy(trans_hbm.at[t], tr32.at[t], tr_sem.at[t]).start()
    stack_copy = pltpu.make_async_copy(basis_hbm, stack, in_sem.at[2])
    stack_copy.start()
    tm_copy = pltpu.make_async_copy(tmat_hbm, tm32, in_sem.at[3])
    tm_copy.start()

    barrier = pltpu.get_barrier_semaphore()

    def greet(target):
        pl.semaphore_signal(barrier, inc=1, device_id={"blk": target}, device_id_type=MESH)

    def plane_peer(d):
        return z * PLANE + (q + d) % PLANE

    def ring_peer(d):
        return ((z + d) % n_ring) * PLANE + q

    for d in range(1, PLANE):
        greet(plane_peer(d))
    for d in range(1, n_ring):
        greet(ring_peer(d))

    @pl.when(far_left)
    def _():
        greet(left)

    @pl.when(far_right)
    def _():
        greet(right)

    first_block = me * n_loc
    for b in range(n_loc):
        keys = []
        for k in range(slots):
            row = nbr_block[b, k] - first_block + n_loc
            keys.append(jnp.where(k < nbr_count[b], nbr_type[b, k] * window + row, -1))
        for t in range(kinds):
            for p in range(b, b + 2 * n_loc + 1):
                hits = [jnp.where(key == t * window + p, 1, 0) for key in keys]
                while len(hits) > 1:
                    hits = [a + c for a, c in zip(hits[::2], hits[1::2])] + (
                        [hits[-1]] if len(hits) % 2 else []
                    )
                weights[(b * kinds + t) * window + p] = hits[0].astype(F32)

    pl.semaphore_wait(
        barrier,
        PLANE + n_ring - 2 + far_left.astype(jnp.int32) + far_right.astype(jnp.int32),
    )

    def halo(step, side, r):
        lo, n = chunks[r]
        to = 0 if side == 0 else 2 * n_loc
        return pltpu.make_async_remote_copy(
            src_ref=wins.at[step, pl.ds(n_loc, n_loc), pl.ds(lo, n)],
            dst_ref=wins.at[step, pl.ds(to, n_loc), pl.ds(lo, n)],
            send_sem=halo_send.at[step, side, r],
            recv_sem=halo_recv.at[step, side, r],
            device_id={"blk": right if side == 0 else left},
            device_id_type=MESH,
        )

    def halo_start(step, r):
        @pl.when(has_right)
        def _():
            halo(step, 0, r).start()

        @pl.when(has_left)
        def _():
            halo(step, 1, r).start()

    def halo_wait(step, r):
        @pl.when(has_left)
        def _():
            halo(step, 0, r).wait_recv()

        @pl.when(has_right)
        def _():
            halo(step, 1, r).wait_recv()

    own.wait()
    for r in range(len(chunks)):
        halo_start(0, r)

    @pl.when(jnp.logical_not(has_left))
    def _():
        wins[0, 0:n_loc] = jnp.zeros((n_loc, coef, sph), F32)
        wins[1, 0:n_loc] = jnp.zeros((n_loc, coef, sph), F32)

    @pl.when(jnp.logical_not(has_right))
    def _():
        wins[0, 2 * n_loc :] = jnp.zeros((n_loc, coef, sph), F32)
        wins[1, 2 * n_loc :] = jnp.zeros((n_loc, coef, sph), F32)

    rows_ref[...] = jnp.zeros_like(rows_ref)
    sum3[...] = jnp.zeros_like(sum3)

    cp_copy.wait()

    def split_coup(t, carry):
        high, low = halves(cp32[t].T)
        cp2[t, 0:sph, 0:sph] = high
        cp2[t, 0:sph, sph:] = low
        cp2[t, sph:, 0:sph] = high
        cp2[t, sph:, sph:] = jnp.zeros_like(low)
        return carry

    lax.fori_loop(0, kinds, split_coup, 0)

    def split_left(x, n):
        if n < LANES:
            x = jnp.concatenate([x, jnp.zeros((coef, LANES - n), F32)], axis=1)
        return halves(x)

    def split_trans(t, carry):
        pltpu.make_async_copy(trans_hbm.at[t], tr32.at[t], tr_sem.at[t]).wait()
        for r, (lo, n) in enumerate(chunks):
            high, low = split_left(tr32[t, :, lo : lo + n], n)
            for i, part in enumerate((high, low, high)):
                at = pl.multiple_of((t * 3 + i) * LANES, LANES)
                tr3[r, :, pl.ds(at, LANES)] = part
        return carry

    lax.fori_loop(0, kinds, split_trans, 0)

    stack_copy.wait()
    pairs = [(i, j) for i in range(n_vec) for j in range(i, n_vec)]

    def gram_step(g, sums):
        at = pl.multiple_of(g * 8, 8)
        sums = list(sums)
        for b in range(n_loc):
            vs = [stack[i, b, pl.ds(at, 8), :] for i in range(n_vec)]
            for c, (i, j) in enumerate(pairs):
                sums[c] = sums[c] + vs[i] * vs[j]
        return tuple(sums)

    gram = lax.fori_loop(
        0, coef // 8, gram_step, tuple(jnp.zeros((8, sph), F32) for _ in pairs)
    )
    for c, (i, j) in enumerate(pairs):
        at = lane_of[i, j]
        rows_ref[at : at + 1, :] = jnp.sum(gram[c], axis=0, keepdims=True)

    tm_copy.wait()

    def split_tmat(t, carry):
        for r, (lo, n) in enumerate(chunks):
            high, low = split_left(tm32[t, :, lo : lo + n], n)
            for i, part in enumerate((high, low, high)):
                at = (r * 3 + i) * LANES
                tm3[t, :, at : at + LANES] = part
        return carry

    lax.fori_loop(0, s_kinds, split_tmat, 0)

    def mix(step, r):
        lo, n = chunks[r]
        for t in range(kinds):
            blocks = []
            for b in range(n_loc):
                total = None
                for p in range(b, b + 2 * n_loc + 1):
                    term = weights[(b * kinds + t) * window + p] * wins[step, p, lo : lo + n, :]
                    total = term if total is None else total + term
                blocks.append(total)
            high, low = halves(jnp.concatenate(blocks, axis=0))
            both = jnp.dot(
                jnp.concatenate([high, low], axis=1), cp2[t], preferred_element_type=F32
            )
            high, low = halves(both[:, :sph] + both[:, sph:])
            for i, part in enumerate((high, high, low)):
                at = (t * 3 + i) * LANES
                for b in range(n_loc):
                    mix3[r % 2, at : at + n, b * sph : (b + 1) * sph] = part[b * n : (b + 1) * n]

    def apply(step):
        halo_wait(step, 0)
        mix(step, 0)
        for r in range(len(chunks)):
            if r + 1 < len(chunks):
                halo_wait(step, r + 1)
                mix(step, r + 1)
            part = jnp.dot(tr3[r], mix3[r % 2], preferred_element_type=F32)
            if r == 0:
                acc[...] = part
            else:
                acc[...] += part
        for r, (lo, n) in enumerate(chunks):
            high, low = halves(acc[lo : lo + n, :])
            for i, part in enumerate((high, high, low)):
                at = (r * 3 + i) * LANES
                sum3[at : at + n, :] = part
        types = jnp.concatenate([sphere_type[b : b + 1, :] for b in range(n_loc)], axis=1)
        for t in range(s_kinds):
            part = jnp.dot(tm3[t], sum3[...], preferred_element_type=F32)
            here = jnp.broadcast_to(types == t, part.shape)
            if t == 0:
                acc[...] = jnp.where(here, part, 0.0)
            else:
                acc[...] = jnp.where(here, part, acc[...])
        for b in range(n_loc):
            image[b] = wins[step, n_loc + b] - acc[:, b * sph : (b + 1) * sph]

    GROUP = 40 if coef % 40 == 0 else 8

    def vector_rows(i, b, at):
        if i < n_vec:
            return stack[i, b, pl.ds(at, GROUP), :]
        return wins[1, n_loc + b, pl.ds(at, GROUP), :]

    def fold(x):
        return jnp.sum(x.reshape(GROUP // 8, 8, sph), axis=0)

    def dots(lefts, right_rows, extra):
        def body(g, sums):
            at = pl.multiple_of(g * GROUP, 8)
            sums = list(sums)
            for b in range(n_loc):
                w = right_rows(b, at)
                for c, i in enumerate(lefts):
                    sums[c] = sums[c] + fold(vector_rows(i, b, at) * w)
                if extra:
                    sums[-1] = sums[-1] + fold(w * w)
            return tuple(sums)

        zero = jnp.zeros((8, sph), F32)
        return lax.fori_loop(
            0, coef // GROUP, body, tuple(zero for _ in range(len(lefts) + int(extra)))
        )

    def lanes_of_rows():
        x = rows_ref[...]
        col = jnp.sum(x, axis=1, keepdims=True)
        row_id = lax.broadcasted_iota(jnp.int32, x.shape, 0)
        lane_id = lax.broadcasted_iota(jnp.int32, x.shape, 1)
        return jnp.sum(jnp.where(row_id == lane_id, col, 0.0), axis=0, keepdims=True)

    def plane_copy(step, d):
        return pltpu.make_async_remote_copy(
            src_ref=plane_buf.at[step, q],
            dst_ref=plane_buf.at[step, q],
            send_sem=plane_send.at[step, d],
            recv_sem=plane_recv.at[step, d],
            device_id={"blk": plane_peer(d)},
            device_id_type=MESH,
        )

    def ring_copy(step, d):
        return pltpu.make_async_remote_copy(
            src_ref=ring_buf.at[step, z],
            dst_ref=ring_buf.at[step, z],
            send_sem=ring_send.at[step, d],
            recv_sem=ring_recv.at[step, d],
            device_id={"blk": ring_peer(d)},
            device_id_type=MESH,
        )

    def all_reduce(step, x):
        plane_buf[step, q] = x
        for d in range(1, PLANE):
            plane_copy(step, d).start()
        for d in range(1, PLANE):
            plane_copy(step, d).wait_recv()
        ring_buf[step, z] = functools.reduce(
            jnp.add, [plane_buf[step, i] for i in range(PLANE)]
        )
        order = sorted(range(1, n_ring), key=lambda d: -min(d, n_ring - d))
        for d in order:
            ring_copy(step, d).start()
        for d in order:
            ring_copy(step, d).wait_recv()
        return functools.reduce(jnp.add, [ring_buf[step, i] for i in range(n_ring)])

    def orthogonal(step, n_used, store):
        sums = dots(range(n_used), lambda b, at: image[b, pl.ds(at, GROUP), :], True)
        for i in range(n_used):
            rows_ref[i : i + 1, :] = jnp.sum(sums[i], axis=0, keepdims=True)
        rows_ref[most : most + 1, :] = jnp.sum(sums[n_used], axis=0, keepdims=True)
        total = all_reduce(step, lanes_of_rows())
        coeffs = total * (1.0 / cells)
        spread = [jnp.broadcast_to(coeffs[:, i : i + 1], (1, LANES)) for i in range(n_used)]

        def factor(which):
            out = jnp.where(which == most, 1.0, 0.0)
            for i in range(n_used):
                out = jnp.where(which == i, spread[i], out)
            return out

        share = total * table[2:3, :].astype(F32)
        share = share * factor(table[0:1, :]) * factor(table[1:2, :])
        squares = jnp.sum(share, axis=1, keepdims=True)
        norm = jnp.sqrt(jnp.maximum(squares, 0.0) * (1.0 / cells) + 1e-6)
        lane = lax.broadcasted_iota(jnp.int32, (1, LANES), 1)
        norm_row = jnp.broadcast_to(norm, (1, LANES))
        hess_ref[step : step + 1, :] = jnp.where(lane == n_used, norm_row, coeffs)
        inverse = jnp.broadcast_to(1.0 / norm_row, (8, LANES))
        wide = [jnp.broadcast_to(s, (8, LANES)) for s in spread]

        def rows(lo, n):
            def body(g, carry):
                at = pl.multiple_of(lo + g * 8, 8)
                for b in range(n_loc):
                    u = image[b, pl.ds(at, 8), :]
                    for i in range(n_used):
                        if i < n_vec:
                            u = u - wide[i] * stack[i, b, pl.ds(at, 8), :]
                        else:
                            u = u - wide[i] * wins[1, n_loc + b, pl.ds(at, 8), :]
                    store(b, at, u * inverse)
                return carry

            lax.fori_loop(0, n // 8, body, 0, unroll=4)

        return rows

    apply(0)

    def store_first(b, at, value):
        wins[1, n_loc + b, pl.ds(at, 8), :] = value

    rows = orthogonal(0, n_vec, store_first)
    for r, (lo, n) in enumerate(chunks):
        rows(lo, n)
        halo_start(1, r)
    out_first = pltpu.make_async_copy(
        wins.at[1, pl.ds(n_loc, n_loc)], new_hbm.at[0], out_sem.at[0]
    )
    out_first.start()

    def first_rows(b, at):
        return wins[1, n_loc + b, pl.ds(at, GROUP), :]

    new_pairs = dots(range(n_vec), first_rows, True)
    for i in range(most):
        at = lane_of[i, n_vec]
        rows_ref[at : at + 1, :] = jnp.sum(new_pairs[i], axis=0, keepdims=True)

    apply(1)

    def store_second(b, at, value):
        image[b, pl.ds(at, 8), :] = value

    rows = orthogonal(1, most, store_second)
    rows(0, coef)
    out_second = pltpu.make_async_copy(image, new_hbm.at[1], out_sem.at[1])
    out_second.start()

    for step in range(2):
        for r in range(len(chunks)):

            @pl.when(has_right)
            def _():
                halo(step, 0, r).wait_send()

            @pl.when(has_left)
            def _():
                halo(step, 1, r).wait_send()

        for d in range(1, PLANE):
            plane_copy(step, d).wait_send()
        for d in range(1, n_ring):
            ring_copy(step, d).wait_send()
    out_first.wait()
    out_second.wait()


def shards(n_blk, basis, nbr_block, nbr_type, nbr_count, sphere_type, trans, coup, tmat):
    n_vec, n_loc, coef, sph = basis.shape
    kinds, s_kinds = trans.shape[0], tmat.shape[0]
    chunks = chunk_rows(coef)
    n_ring = n_blk // PLANE
    table, lane_of, used = lane_tables(n_vec + 1)
    cells = float(n_blk * n_loc * coef * sph)
    any_space = pl.BlockSpec(memory_space=pl.ANY)
    smem = pl.BlockSpec(memory_space=pltpu.SMEM)
    vmem = pl.BlockSpec(memory_space=pltpu.VMEM)
    dma = pltpu.SemaphoreType.DMA
    wide = n_loc * sph
    new, hess = pl.pallas_call(
        functools.partial(kernel, n_blk, cells, lane_of),
        out_shape=(
            jax.ShapeDtypeStruct((2, n_loc, coef, sph), F32),
            jax.ShapeDtypeStruct((8, LANES), F32),
        ),
        in_specs=[any_space, smem, smem, smem, vmem, vmem, any_space, any_space, any_space],
        out_specs=(any_space, vmem),
        scratch_shapes=[
            pltpu.VMEM((2, 3 * n_loc, coef, sph), F32),
            pltpu.VMEM((n_vec, n_loc, coef, sph), F32),
            pltpu.VMEM(trans.shape, F32),
            pltpu.VMEM(tmat.shape, F32),
            pltpu.VMEM(coup.shape, F32),
            pltpu.VMEM((len(chunks), coef, kinds * 3 * LANES), BF16),
            pltpu.VMEM((s_kinds, coef, len(chunks) * 3 * LANES), BF16),
            pltpu.VMEM((kinds, 2 * sph, 2 * sph), BF16),
            pltpu.VMEM((2, kinds * 3 * LANES, wide), BF16),
            pltpu.VMEM((len(chunks) * 3 * LANES, wide), BF16),
            pltpu.VMEM((coef, wide), F32),
            pltpu.VMEM((n_loc, coef, sph), F32),
            pltpu.VMEM(((used + 7) // 8 * 8, LANES), F32),
            pltpu.VMEM((2, PLANE, 1, LANES), F32),
            pltpu.VMEM((2, n_ring, 1, LANES), F32),
            pltpu.SMEM((n_loc * kinds * 3 * n_loc,), F32),
            dma((kinds,)),
            dma((4,)),
            dma((2,)),
            dma((2, 2, len(chunks))),
            dma((2, 2, len(chunks))),
            dma((2, PLANE)),
            dma((2, PLANE)),
            dma((2, n_ring)),
            dma((2, n_ring)),
        ],
        compiler_params=pltpu.CompilerParams(
            collective_id=0, has_side_effects=True, vmem_limit_bytes=60 * 1024 * 1024
        ),
    )(
        basis,
        nbr_block,
        nbr_type,
        nbr_count,
        sphere_type,
        jnp.asarray(table),
        trans,
        coup,
        tmat,
    )
    return new, hess[0, : n_vec + 1], hess[1, : n_vec + 2]


def solution(mesh):
    return jax.shard_map(
        functools.partial(shards, mesh.shape["blk"]),
        mesh=mesh,
        in_specs=(
            P(None, GB, None, None),
            P(GB, None),
            P(GB, None),
            P(GB),
            P(GB, None),
            P(),
            P(),
            P(),
        ),
        out_specs=(P(None, GB, None, None), P("groups"), P("groups")),
        check_vma=False,
    )
```

profile of v0, /device:TPU:40, one launch (start us, length us, event | category | flops | bytes accessed | tf_op | source)
XLA Modules:
  0.0 90.1 jit_solution(10337778665895637538)
XLA Ops:
  0.6 84.9 %shard_map.112 = (f32[2,2,480,128]{3,2,1,0:T(8,128)}, f32[8,128]{1,0:T(8,128)}) custom-call(f32[8,2,480,128]{3,2,1,0:T(8,128)} %basis_hbm.1, s32[2,14]{1,0:T(2,128)} %nbr_block.1, s32[2,14]{1,0:T(2,128)} %nbr_type.1, s32[2]{0:T(128)} %nbr_count.1, s32[2,128]{1,0:T(2,128)} %sphere_type.1, s32[8,128]{1,0:T(8,128)} %constant.2.clone.table, ...), custom_call_target="tpu_custom_call" | custom-call | tf_op jit(solution)/shard_map/pallas_call | solution.py:489
  85.5 1.2 %slice_bitcast_fusion = f32[10]{0:T(128)} fusion(f32[8,128]{1,0:T(8,128)} %get-tuple-element.6), kind=kLoop, calls=%fused_computation | loop fusion | bytes 80 | tf_op jit(solution)/shard_map/squeeze | solution.py:538
  86.7 1.2 %slice_bitcast_fusion.1 = f32[9]{0:T(128)} fusion(f32[8,128]{1,0:T(8,128)} %get-tuple-element.6), kind=kLoop, calls=%fused_computation.1 | loop fusion | bytes 72 | tf_op jit(solution)/shard_map/squeeze | solution.py:538
  87.9 2.2 %copy.13 = f32[2,2,480,128]{3,2,1,0:T(8,128)} copy(f32[2,2,480,128]{3,2,1,0:T(8,128)} %get-tuple-element.10) | data formatting | bytes 1966080
where the time goes:
time: 90.4 us; the launch traced here: 90.1 us
  Pallas kernels  84.9 us (94%)
  local copies, waits for them, and re-layouts  4.58 us (5%)
    pallas_call x1, Pallas kernels, shards(): pl.pallas_call(functools.partial(kernel, n_blk, cells, lane_of), out_shap...  84.9 us
    squeeze x2, local copies, waits for them, and re-layouts, shards(): return (new, hess[0, :n_vec + 1], hess[1, :n_vec + 2])  2.37 us
    unnamed x1, local copies, waits for them, and re-layouts  2.21 us

commit v1 on v0

v1 whole, which is shorter than its diff:
```python
import functools

import jax
import jax.numpy as jnp
import numpy as np
from jax import lax
from jax.experimental import pallas as pl
from jax.experimental.pallas import tpu as pltpu
from jax.sharding import PartitionSpec as P

GB = ("groups", "blk")
PLANE = 8
LANES = 128
F32 = jnp.float32
BF16 = jnp.bfloat16
MESH = pl.DeviceIdType.MESH


def chunk_rows(coef):
    return [(c, min(LANES, coef - c)) for c in range(0, coef, LANES)]


def lane_tables(most):
    one = most
    table = np.zeros((8, LANES), np.int32)
    table[0:2, :] = most + 1
    lane_of = {}
    for i in range(most):
        table[0:3, i] = (i, one, -2)
    table[0:3, most] = (one, one, 1)
    at = most + 1
    for i in range(most):
        for j in range(i, most):
            table[0:3, at] = (i, j, 1 if i == j else 2)
            lane_of[i, j] = at
            at += 1
    return table, lane_of, at


def halves(x):
    high = x.astype(BF16)
    return high, (x - high.astype(F32)).astype(BF16)


def kernel(
    n_blk,
    cells,
    lane_of,
    basis_hbm,
    nbr_block_hbm,
    nbr_type_hbm,
    nbr_count_hbm,
    sphere_type_hbm,
    table_hbm,
    trans_hbm,
    coup_hbm,
    tmat_hbm,
    new_ref,
    hess_ref,
    nbr_block,
    nbr_type,
    nbr_count,
    sphere_type,
    table,
    weights,
    wins,
    stack,
    tr32,
    tm32,
    cp32,
    tr3,
    tm3,
    cp2,
    mix3,
    sum3,
    acc,
    image,
    rows_ref,
    plane_buf,
    ring_buf,
    tr_sem,
    in_sem,
    halo_send,
    halo_recv,
    plane_send,
    plane_recv,
    ring_send,
    ring_recv,
):
    n_vec, n_loc, coef, sph = basis_hbm.shape
    kinds = trans_hbm.shape[0]
    s_kinds = tmat_hbm.shape[0]
    slots = nbr_block_hbm.shape[1]
    most = n_vec + 1
    chunks = chunk_rows(coef)
    n_ring = n_blk // PLANE
    window = 3 * n_loc

    me = lax.axis_index("blk")
    z = me // PLANE
    q = me % PLANE
    left, right = me - 1, me + 1
    has_left, has_right = me > 0, me < n_blk - 1
    far_left = jnp.logical_and(q == 0, has_left)
    far_right = jnp.logical_and(q == PLANE - 1, has_right)

    own = pltpu.make_async_copy(
        basis_hbm.at[n_vec - 1], wins.at[0, pl.ds(n_loc, n_loc)], in_sem.at[0]
    )
    own.start()
    small = [
        pltpu.make_async_copy(src, dst, in_sem.at[4 + i])
        for i, (src, dst) in enumerate(
            (
                (nbr_block_hbm, nbr_block),
                (nbr_type_hbm, nbr_type),
                (nbr_count_hbm, nbr_count),
                (sphere_type_hbm, sphere_type),
                (table_hbm, table),
            )
        )
    ]
    for copy in small:
        copy.start()
    cp_copy = pltpu.make_async_copy(coup_hbm, cp32, in_sem.at[1])
    cp_copy.start()

    def trans_copy(r):
        lo, n = chunks[r]
        return pltpu.make_async_copy(
            trans_hbm.at[:, :, pl.ds(lo, n)], tr32.at[:, :, pl.ds(lo, n)], tr_sem.at[r]
        )

    for r in range(len(chunks)):
        trans_copy(r).start()
    stack_copy = pltpu.make_async_copy(basis_hbm, stack, in_sem.at[2])
    stack_copy.start()
    tm_copy = pltpu.make_async_copy(tmat_hbm, tm32, in_sem.at[3])
    tm_copy.start()

    barrier = pltpu.get_barrier_semaphore()

    def greet(target):
        pl.semaphore_signal(barrier, inc=1, device_id={"blk": target}, device_id_type=MESH)

    def plane_peer(d):
        return z * PLANE + (q + d) % PLANE

    def ring_peer(d):
        return ((z + d) % n_ring) * PLANE + q

    for d in range(1, PLANE):
        greet(plane_peer(d))
    for d in range(1, n_ring):
        greet(ring_peer(d))

    @pl.when(far_left)
    def _():
        greet(left)

    @pl.when(far_right)
    def _():
        greet(right)

    pl.semaphore_wait(
        barrier,
        PLANE + n_ring - 2 + far_left.astype(jnp.int32) + far_right.astype(jnp.int32),
    )

    def halo(step, side, r):
        lo, n = chunks[r]
        to = 0 if side == 0 else 2 * n_loc
        return pltpu.make_async_remote_copy(
            src_ref=wins.at[step, pl.ds(n_loc, n_loc), pl.ds(lo, n)],
            dst_ref=wins.at[step, pl.ds(to, n_loc), pl.ds(lo, n)],
            send_sem=halo_send.at[step, side, r],
            recv_sem=halo_recv.at[step, side, r],
            device_id={"blk": right if side == 0 else left},
            device_id_type=MESH,
        )

    def halo_start(step, r):
        @pl.when(has_right)
        def _():
            halo(step, 0, r).start()

        @pl.when(has_left)
        def _():
            halo(step, 1, r).start()

    def halo_wait(step, r):
        @pl.when(has_left)
        def _():
            halo(step, 0, r).wait_recv()

        @pl.when(has_right)
        def _():
            halo(step, 1, r).wait_recv()

    own.wait()
    for r in range(len(chunks)):
        halo_start(0, r)

    @pl.when(jnp.logical_not(has_left))
    def _():
        wins[0, 0:n_loc] = jnp.zeros((n_loc, coef, sph), F32)
        wins[1, 0:n_loc] = jnp.zeros((n_loc, coef, sph), F32)

    @pl.when(jnp.logical_not(has_right))
    def _():
        wins[0, 2 * n_loc :] = jnp.zeros((n_loc, coef, sph), F32)
        wins[1, 2 * n_loc :] = jnp.zeros((n_loc, coef, sph), F32)

    for copy in small:
        copy.wait()
    first_block = me * n_loc
    slot_id = lax.broadcasted_iota(jnp.int32, (1, slots), 1)
    use_id = lax.broadcasted_iota(jnp.int32, (kinds * window, slots), 0)
    for b in range(n_loc):
        use = nbr_type[b : b + 1, :] * window + (nbr_block[b : b + 1, :] - first_block + n_loc)
        use = jnp.where(slot_id < nbr_count[b], use, -1)
        hits = jnp.sum(jnp.where(use_id == use, 1.0, 0.0), axis=1, keepdims=True)
        weights[b] = jnp.broadcast_to(hits, (kinds * window, LANES))

    rows_ref[...] = jnp.zeros_like(rows_ref)
    sum3[...] = jnp.zeros_like(sum3)

    cp_copy.wait()

    def split_coup(t, carry):
        high, low = halves(cp32[t].T)
        cp2[t, 0, 0:sph] = high
        cp2[t, 0, sph:] = high
        cp2[t, 1, 0:sph] = low
        cp2[t, 1, sph:] = jnp.zeros_like(low)
        return carry

    lax.fori_loop(0, kinds, split_coup, 0, unroll=4)

    def split_left(x, n):
        if n < LANES:
            x = jnp.concatenate([x, jnp.zeros((coef, LANES - n), F32)], axis=1)
        return halves(x)

    def split_trans(r):
        lo, n = chunks[r]
        for t in range(kinds):
            high, low = split_left(tr32[t, :, lo : lo + n], n)
            tr3[r, 0, t] = high
            tr3[r, 1, t] = low

    def split_tmat():
        for t in range(s_kinds):
            for r, (lo, n) in enumerate(chunks):
                high, low = split_left(tm32[t, :, lo : lo + n], n)
                tm3[t, 0, r] = high
                tm3[t, 1, r] = low

    depth = len(chunks) * LANES
    pairs = [(i, j) for i in range(n_vec) for j in range(i, n_vec)]

    def gram_step(g, sums):
        at = pl.multiple_of(g * 8, 8)
        sums = list(sums)
        for b in range(n_loc):
            vs = [stack[i, b, pl.ds(at, 8), :] for i in range(n_vec)]
            for c, (i, j) in enumerate(pairs):
                sums[c] = sums[c] + vs[i] * vs[j]
        return tuple(sums)

    def basis_pairs():
        gram = lax.fori_loop(
            0, coef // 8, gram_step, tuple(jnp.zeros((8, sph), F32) for _ in pairs)
        )
        for c, (i, j) in enumerate(pairs):
            at = lane_of[i, j]
            rows_ref[at : at + 1, :] = jnp.sum(gram[c], axis=0, keepdims=True)

    def three(left, right):
        high, low = right
        part = jnp.dot(left[0], high, preferred_element_type=F32)
        part += jnp.dot(left[1], high, preferred_element_type=F32)
        part += jnp.dot(left[0], low, preferred_element_type=F32)
        return part

    def wide_left(ref, lead, count, rows):
        return [
            jnp.concatenate([ref[(*lead, i, k, rows)] for k in range(count)], axis=1)
            for i in range(2)
        ]

    def wide_right(ref, lead):
        return [
            jnp.concatenate([ref[(*lead, i, b)] for b in range(n_loc)], axis=1)
            for i in range(2)
        ]

    half = coef // 2

    def product(r):
        for lo in (0, half):
            left = wide_left(tr3, (r,), kinds, slice(lo, lo + half))
            part = three(left, wide_right(mix3, (r % 2,)))
            if r == 0:
                acc[lo : lo + half] = part
            else:
                acc[lo : lo + half] += part

    def mix(step, r):
        lo, n = chunks[r]
        for t in range(kinds):
            blocks = []
            for b in range(n_loc):
                total = None
                for p in range(b, b + 2 * n_loc + 1):
                    c = t * window + p
                    term = weights[b, c : c + 1, :] * wins[step, p, lo : lo + n, :]
                    total = term if total is None else total + term
                blocks.append(total)
            high, low = halves(jnp.concatenate(blocks, axis=0))
            both = jnp.dot(
                jnp.concatenate([high, low], axis=1),
                jnp.concatenate([cp2[t, 0], cp2[t, 1]], axis=1),
                preferred_element_type=F32,
            )
            high, low = halves(both[:, :sph] + both[:, sph:])
            for i, part in enumerate((high, low)):
                for b in range(n_loc):
                    mix3[r % 2, i, b, t * LANES : t * LANES + n] = part[b * n : (b + 1) * n]

    def apply(step):
        last = len(chunks) - 1
        for r in range(len(chunks)):
            if step == 0:
                trans_copy(r).wait()
            halo_wait(step, r)
            if step == 0:
                split_trans(r)
            mix(step, r)
            if r > 0:
                product(r - 1)
        if step == 0:
            tm_copy.wait()
            stack_copy.wait()

        @pl.when(me >= 0)
        def _():
            product(last)
            if step == 0:
                split_tmat()

        for lo, n in chunks:
            high, low = halves(acc[lo : lo + n, :])
            for b in range(n_loc):
                sum3[0, b, lo : lo + n] = high[:, b * sph : (b + 1) * sph]
                sum3[1, b, lo : lo + n] = low[:, b * sph : (b + 1) * sph]
        types = jnp.concatenate([sphere_type[b : b + 1, :] for b in range(n_loc)], axis=1)

        def scatter(i, carry):
            for t in (2 * i, 2 * i + 1):
                part = three(
                    wide_left(tm3, (t,), len(chunks), slice(None)), wide_right(sum3, ())
                )
                here = jnp.broadcast_to(types == t, part.shape)
                acc[...] = jnp.where(here, part, acc[...])
            return carry

        lax.fori_loop(0, s_kinds // 2, scatter, 0)
        for b in range(n_loc):
            image[b] = wins[step, n_loc + b] - acc[:, b * sph : (b + 1) * sph]

    GROUP = 40 if coef % 40 == 0 else 8

    def vector_rows(i, b, at):
        if i < n_vec:
            return stack[i, b, pl.ds(at, GROUP), :]
        return wins[1, n_loc + b, pl.ds(at, GROUP), :]

    def fold(x):
        return jnp.sum(x.reshape(GROUP // 8, 8, sph), axis=0)

    def dots(lefts, right_rows, extra):
        def body(g, sums):
            at = pl.multiple_of(g * GROUP, 8)
            sums = list(sums)
            for b in range(n_loc):
                w = right_rows(b, at)
                for c, i in enumerate(lefts):
                    sums[c] = sums[c] + fold(vector_rows(i, b, at) * w)
                if extra:
                    sums[-1] = sums[-1] + fold(w * w)
            return tuple(sums)

        zero = jnp.zeros((8, sph), F32)
        return lax.fori_loop(
            0, coef // GROUP, body, tuple(zero for _ in range(len(lefts) + int(extra)))
        )

    def lanes_of_rows():
        x = rows_ref[...]
        col = jnp.sum(x, axis=1, keepdims=True)
        row_id = lax.broadcasted_iota(jnp.int32, x.shape, 0)
        lane_id = lax.broadcasted_iota(jnp.int32, x.shape, 1)
        return jnp.sum(jnp.where(row_id == lane_id, col, 0.0), axis=0, keepdims=True)

    def plane_copy(step, d):
        return pltpu.make_async_remote_copy(
            src_ref=plane_buf.at[step, q],
            dst_ref=plane_buf.at[step, q],
            send_sem=plane_send.at[step, d],
            recv_sem=plane_recv.at[step, d],
            device_id={"blk": plane_peer(d)},
            device_id_type=MESH,
        )

    def ring_copy(step, d):
        return pltpu.make_async_remote_copy(
            src_ref=ring_buf.at[step, z],
            dst_ref=ring_buf.at[step, z],
            send_sem=ring_send.at[step, d],
            recv_sem=ring_recv.at[step, d],
            device_id={"blk": ring_peer(d)},
            device_id_type=MESH,
        )

    def all_reduce(step, x, meanwhile):
        plane_buf[step, q] = x
        for d in range(1, PLANE):
            plane_copy(step, d).start()
        for d in range(1, PLANE):
            plane_copy(step, d).wait_recv()
        ring_buf[step, z] = functools.reduce(
            jnp.add, [plane_buf[step, i] for i in range(PLANE)]
        )
        order = sorted(range(1, n_ring), key=lambda d: -min(d, n_ring - d))
        for d in order:
            ring_copy(step, d).start()
        meanwhile()
        for d in order:
            ring_copy(step, d).wait_recv()
        return functools.reduce(jnp.add, [ring_buf[step, i] for i in range(n_ring)])

    def reduced(step, n_used, meanwhile):
        sums = dots(range(n_used), lambda b, at: image[b, pl.ds(at, GROUP), :], True)
        for i in range(n_used):
            rows_ref[i : i + 1, :] = jnp.sum(sums[i], axis=0, keepdims=True)
        rows_ref[most : most + 1, :] = jnp.sum(sums[n_used], axis=0, keepdims=True)
        return all_reduce(step, lanes_of_rows(), meanwhile) * (1.0 / cells)

    def spread(row, i):
        return jnp.broadcast_to(row[:, i : i + 1], (1, LANES))

    def tall(row):
        return jnp.broadcast_to(row, (8, LANES))

    def vector8(i, b, at):
        if i < n_vec:
            return stack[i, b, pl.ds(at, 8), :]
        return wins[1, n_loc + b, pl.ds(at, 8), :]

    def combine(shares, scale, store, lo, n):
        def body(g, carry):
            at = pl.multiple_of(lo + g * 8, 8)
            for b in range(n_loc):
                u = image[b, pl.ds(at, 8), :]
                for i, share in enumerate(shares):
                    u = u - share * vector8(i, b, at)
                store(b, at, u * scale)
            return carry

        lax.fori_loop(0, n // 8, body, 0, unroll=4)

    lane = lax.broadcasted_iota(jnp.int32, (1, LANES), 1)

    apply(0)
    means = reduced(0, n_vec, basis_pairs)
    first_row = means
    size2 = spread(means, most) + 1e-6
    size = jnp.sqrt(size2)
    shares = [tall(spread(means, i)) for i in range(n_vec)]
    scale = tall(1.0 / size)

    def store_first(b, at, value):
        wins[1, n_loc + b, pl.ds(at, 8), :] = value

    for r, (lo, n) in enumerate(chunks):
        combine(shares, scale, store_first, lo, n)
        halo_start(1, r)

    def first_rows(b, at):
        return wins[1, n_loc + b, pl.ds(at, GROUP), :]

    new_pairs = dots(range(n_vec), first_rows, True)
    for i in range(most):
        at = lane_of[i, n_vec]
        rows_ref[at : at + 1, :] = jnp.sum(new_pairs[i], axis=0, keepdims=True)

    apply(1)
    means = reduced(1, most, lambda: None)
    norm1 = jnp.sqrt(size2 * spread(means, lane_of[n_vec, n_vec]) + 1e-6)
    ratio = size / norm1
    parts = [spread(means, i) for i in range(n_vec)]
    parts.append(ratio * ratio * spread(means, n_vec))

    def factor(which):
        out = jnp.where(which == most, 1.0, 0.0)
        for i in range(most):
            out = jnp.where(which == i, parts[i], out)
        return out

    share = means * table[2:3, :].astype(F32)
    share = share * factor(table[0:1, :]) * factor(table[1:2, :])
    squares = jnp.broadcast_to(jnp.sum(share, axis=1, keepdims=True), (1, LANES))
    norm2 = jnp.sqrt(ratio * ratio * jnp.maximum(squares, 0.0) + 1e-6)
    hess_ref[0:1, :] = jnp.where(lane == n_vec, norm1, first_row)
    second_row = ratio * jnp.where(lane == n_vec, ratio * means, means)
    hess_ref[1:2, :] = jnp.where(lane == most, norm2, second_row)

    grow = tall(ratio)

    def store_second(b, at, value):
        new_ref[1, b, pl.ds(at, 8), :] = value
        new_ref[0, b, pl.ds(at, 8), :] = vector8(n_vec, b, at) * grow

    combine([tall(p) for p in parts], tall(ratio / norm2), store_second, 0, coef)

    for step in range(2):
        for r in range(len(chunks)):

            @pl.when(has_right)
            def _():
                halo(step, 0, r).wait_send()

            @pl.when(has_left)
            def _():
                halo(step, 1, r).wait_send()

        for d in range(1, PLANE):
            plane_copy(step, d).wait_send()
        for d in range(1, n_ring):
            ring_copy(step, d).wait_send()


def finish(new_in, hess, new_out, first, second, sem):
    store = pltpu.make_async_copy(new_in, new_out, sem)
    store.start()
    first[...] = hess[0, : first.shape[0]]
    second[...] = hess[1, : second.shape[0]]
    store.wait()


def shards(n_blk, basis, nbr_block, nbr_type, nbr_count, sphere_type, trans, coup, tmat):
    n_vec, n_loc, coef, sph = basis.shape
    kinds, s_kinds = trans.shape[0], tmat.shape[0]
    chunks = chunk_rows(coef)
    n_ring = n_blk // PLANE
    table, lane_of, used = lane_tables(n_vec + 1)
    cells = float(n_blk * n_loc * coef * sph)
    hbm = pl.BlockSpec(memory_space=pltpu.HBM)
    vmem = pl.BlockSpec(memory_space=pltpu.VMEM)
    dma = pltpu.SemaphoreType.DMA
    wide = n_loc * sph
    in_hbm = functools.partial(pltpu.with_memory_space_constraint, memory_space=pltpu.HBM)
    new, hess = pl.pallas_call(
        functools.partial(kernel, n_blk, cells, lane_of),
        out_shape=(
            jax.ShapeDtypeStruct((2, n_loc, coef, sph), F32),
            jax.ShapeDtypeStruct((8, LANES), F32),
        ),
        in_specs=[hbm] * 9,
        out_specs=(vmem, vmem),
        scratch_shapes=[
            pltpu.VMEM(nbr_block.shape, jnp.int32),
            pltpu.VMEM(nbr_type.shape, jnp.int32),
            pltpu.SMEM(nbr_count.shape, jnp.int32),
            pltpu.VMEM(sphere_type.shape, jnp.int32),
            pltpu.VMEM(table.shape, jnp.int32),
            pltpu.VMEM((n_loc, kinds * 3 * n_loc, LANES), F32),
            pltpu.VMEM((2, 3 * n_loc, coef, sph), F32),
            pltpu.VMEM((n_vec, n_loc, coef, sph), F32),
            pltpu.VMEM(trans.shape, F32),
            pltpu.VMEM(tmat.shape, F32),
            pltpu.VMEM(coup.shape, F32),
            pltpu.VMEM((len(chunks), 2, kinds, coef, LANES), BF16),
            pltpu.VMEM((s_kinds, 2, len(chunks), coef, LANES), BF16),
            pltpu.VMEM((kinds, 2, 2 * sph, sph), BF16),
            pltpu.VMEM((2, 2, n_loc, kinds * LANES, sph), BF16),
            pltpu.VMEM((2, n_loc, len(chunks) * LANES, sph), BF16),
            pltpu.VMEM((coef, wide), F32),
            pltpu.VMEM((n_loc, coef, sph), F32),
            pltpu.VMEM(((used + 7) // 8 * 8, LANES), F32),
            pltpu.VMEM((2, PLANE, 1, LANES), F32),
            pltpu.VMEM((2, n_ring, 1, LANES), F32),
            dma((len(chunks),)),
            dma((9,)),
            dma((2, 2, len(chunks))),
            dma((2, 2, len(chunks))),
            dma((2, PLANE)),
            dma((2, PLANE)),
            dma((2, n_ring)),
            dma((2, n_ring)),
        ],
        compiler_params=pltpu.CompilerParams(
            collective_id=0, has_side_effects=True, vmem_limit_bytes=52 * 1024 * 1024
        ),
    )(
        *map(
            in_hbm,
            (
                basis,
                nbr_block,
                nbr_type,
                nbr_count,
                sphere_type,
                jnp.asarray(table),
                trans,
                coup,
                tmat,
            ),
        )
    )
    return pl.pallas_call(
        finish,
        out_shape=(
            jax.ShapeDtypeStruct(new.shape, F32),
            jax.ShapeDtypeStruct((n_vec + 1,), F32),
            jax.ShapeDtypeStruct((n_vec + 2,), F32),
        ),
        in_specs=[vmem, vmem],
        out_specs=(hbm, vmem, vmem),
        scratch_shapes=[dma],
        compiler_params=pltpu.CompilerParams(vmem_limit_bytes=4 * 1024 * 1024),
    )(new, hess)


def solution(mesh):
    return jax.shard_map(
        functools.partial(shards, mesh.shape["blk"]),
        mesh=mesh,
        in_specs=(
            P(None, GB, None, None),
            P(GB, None),
            P(GB, None),
            P(GB),
            P(GB, None),
            P(),
            P(),
            P(),
        ),
        out_specs=(P(None, GB, None, None), P("groups"), P("groups")),
        check_vma=False,
    )
```

time: 90.4 us -> 79.1 us (0.87)
  Pallas kernels: 84.9 us -> 78.2 us
  local copies, waits for them, and re-layouts: 4.58 us -> 0 us
    pallas_call x1, Pallas kernels: 84.9 us -> 76.7 us  [shards(): pl.pallas_call(functools.partial(kernel, n_blk, cells, lane_of), out_shap...]
    squeeze x2 -> x0, local copies, waits for them, and re-layouts: 2.37 us -> none  [shards(): return (new, hess[0, :n_vec + 1], hess[1, :n_vec + 2])]
    unnamed x1 -> x0, local copies, waits for them, and re-layouts: 2.21 us -> none
    pallas_call x0 -> x1, Pallas kernels: none -> 1.47 us  [shards(): pl.pallas_call(finish, out_shape=(jax.ShapeDtypeStruct(new.shape, F32), j...]
where the time goes in v1:
time: 79.1 us; the launch traced here: 79 us
  Pallas kernels  78.2 us (99%)
  between operations  0.8 us (1%)
    pallas_call x1, Pallas kernels, shards(): pl.pallas_call(functools.partial(kernel, n_blk, cells, lane_of), out_shap...  76.7 us

profile of v1, /device:TPU:40, one launch (start us, length us, event | category | flops | bytes accessed | tf_op | source)
XLA Modules:
  0.0 79.0 jit_solution(11267156995423234078)
XLA Ops:
  0.6 76.7 %shard_map.112 = (f32[2,2,480,128]{3,2,1,0:T(8,128)S(1)}, f32[8,128]{1,0:T(8,128)S(1)}) custom-call(f32[8,2,480,128]{3,2,1,0:T(8,128)} %basis_hbm.1, s32[2,14]{1,0:T(2,128)} %nbr_block_hbm.1, s32[2,14]{1,0:T(2,128)} %nbr_type_hbm.1, s32[2]{0:T(128)} %nbr_count_hbm.1, s32[2,128]{1,0:T(2,128)} %sphere_type_hbm.1, s32[8,128]{1,0:T(8,128)} %constant.2.clone.table_hbm, ...), custom_call_target="tpu_custom_call" | custom-call | tf_op jit(solution)/shard_map/pallas_call | solution.py:564
  77.3 1.5 %shard_map.113 = (f32[2,2,480,128]{3,2,1,0:T(8,128)}, f32[9]{0:T(128)}, f32[10]{0:T(128)}) custom-call(f32[2,2,480,128]{3,2,1,0:T(8,128)S(1)} %get-tuple-element.5.new_in, f32[8,128]{1,0:T(8,128)S(1)} %get-tuple-element.6.hess), custom_call_target="tpu_custom_call" | custom-call | tf_op jit(solution)/shard_map/pallas_call | solution.py:622

commit v2 on v1

--- a/solution.py
+++ b/solution.py
@@ -17,7 +17,8 @@
 
 
 def chunk_rows(coef):
-    return [(c, min(LANES, coef - c)) for c in range(0, coef, LANES)]
+    parts = [(c, min(LANES, coef - c)) for c in range(0, coef, LANES)]
+    return parts[-1:] + parts[:-1]
 
 
 def lane_tables(most):
@@ -86,6 +87,7 @@
     plane_recv,
     ring_send,
     ring_recv,
+    far_sem,
 ):
     n_vec, n_loc, coef, sph = basis_hbm.shape
     kinds = trans_hbm.shape[0]
@@ -108,6 +110,45 @@
         basis_hbm.at[n_vec - 1], wins.at[0, pl.ds(n_loc, n_loc)], in_sem.at[0]
     )
     own.start()
+    barrier = pltpu.get_barrier_semaphore()
+
+    def signal(sem, target):
+        pl.semaphore_signal(sem, inc=1, device_id={"blk": target}, device_id_type=MESH)
+
+    def plane_peer(d):
+        return z * PLANE + (q + d) % PLANE
+
+    def ring_peer(d):
+        return ((z + d) % n_ring) * PLANE + q
+
+    for d in range(1, PLANE):
+        signal(barrier, plane_peer(d))
+    for d in (1, n_ring - 1):
+        signal(barrier, ring_peer(d))
+
+    @pl.when(far_left)
+    def _():
+        signal(barrier, left)
+
+    @pl.when(far_right)
+    def _():
+        signal(barrier, right)
+
+    reach = [1]
+    while 2 * reach[-1] < n_ring:
+        reach.append(2 * reach[-1])
+    rounds = len(reach) - 1
+
+    def far_signal(i):
+        if i < rounds:
+            for d in (reach[i], n_ring - reach[i]):
+                signal(far_sem.at[i], ring_peer(d))
+
+    def far_round(i):
+        if i < rounds:
+            pl.semaphore_wait(far_sem.at[i], 2)
+            far_signal(i + 1)
+
     small = [
         pltpu.make_async_copy(src, dst, in_sem.at[4 + i])
         for i, (src, dst) in enumerate(
@@ -133,39 +174,10 @@
 
     for r in range(len(chunks)):
         trans_copy(r).start()
+    tm_copy = pltpu.make_async_copy(tmat_hbm, tm32, in_sem.at[3])
+    tm_copy.start()
     stack_copy = pltpu.make_async_copy(basis_hbm, stack, in_sem.at[2])
     stack_copy.start()
-    tm_copy = pltpu.make_async_copy(tmat_hbm, tm32, in_sem.at[3])
-    tm_copy.start()
-
-    barrier = pltpu.get_barrier_semaphore()
-
-    def greet(target):
-        pl.semaphore_signal(barrier, inc=1, device_id={"blk": target}, device_id_type=MESH)
-
-    def plane_peer(d):
-        return z * PLANE + (q + d) % PLANE
-
-    def ring_peer(d):
-        return ((z + d) % n_ring) * PLANE + q
-
-    for d in range(1, PLANE):
-        greet(plane_peer(d))
-    for d in range(1, n_ring):
-        greet(ring_peer(d))
-
-    @pl.when(far_left)
-    def _():
-        greet(left)
-
-    @pl.when(far_right)
-    def _():
-        greet(right)
-
-    pl.semaphore_wait(
-        barrier,
-        PLANE + n_ring - 2 + far_left.astype(jnp.int32) + far_right.astype(jnp.int32),
-    )
 
     def halo(step, side, r):
         lo, n = chunks[r]
@@ -197,9 +209,13 @@
         def _():
             halo(step, 1, r).wait_recv()
 
+    pl.semaphore_wait(
+        barrier, PLANE + 1 + far_left.astype(jnp.int32) + far_right.astype(jnp.int32)
+    )
     own.wait()
     for r in range(len(chunks)):
         halo_start(0, r)
+    far_signal(0)
 
     @pl.when(jnp.logical_not(has_left))
     def _():
@@ -224,6 +240,7 @@
 
     rows_ref[...] = jnp.zeros_like(rows_ref)
     sum3[...] = jnp.zeros_like(sum3)
+    mix3[0] = jnp.zeros_like(mix3[0])
 
     cp_copy.wait()
 
@@ -251,10 +268,10 @@
 
     def split_tmat():
         for t in range(s_kinds):
-            for r, (lo, n) in enumerate(chunks):
+            for lo, n in chunks:
                 high, low = split_left(tm32[t, :, lo : lo + n], n)
-                tm3[t, 0, r] = high
-                tm3[t, 1, r] = low
+                tm3[t, 0, lo // LANES] = high
+                tm3[t, 1, lo // LANES] = low
 
     depth = len(chunks) * LANES
     pairs = [(i, j) for i in range(n_vec) for j in range(i, n_vec)]
@@ -331,23 +348,16 @@
     def apply(step):
         last = len(chunks) - 1
         for r in range(len(chunks)):
-            if step == 0:
-                trans_copy(r).wait()
+            if step == 0 and r > 0:
+                far_round(r - 1)
             halo_wait(step, r)
-            if step == 0:
-                split_trans(r)
             mix(step, r)
             if r > 0:
                 product(r - 1)
-        if step == 0:
-            tm_copy.wait()
-            stack_copy.wait()
 
         @pl.when(me >= 0)
         def _():
             product(last)
-            if step == 0:
-                split_tmat()
 
         for lo, n in chunks:
             high, low = halves(acc[lo : lo + n, :])
@@ -472,7 +482,14 @@
 
     lane = lax.broadcasted_iota(jnp.int32, (1, LANES), 1)
 
+    for r in range(len(chunks)):
+        trans_copy(r).wait()
+        split_trans(r)
+    tm_copy.wait()
+    split_tmat()
+
     apply(0)
+    stack_copy.wait()
     means = reduced(0, n_vec, basis_pairs)
     first_row = means
     size2 = spread(means, most) + 1e-6
@@ -599,6 +616,7 @@
             dma((2, PLANE)),
             dma((2, n_ring)),
             dma((2, n_ring)),
+            pltpu.SemaphoreType.REGULAR((max(1, n_ring.bit_length()),)),
         ],
         compiler_params=pltpu.CompilerParams(
             collective_id=0, has_side_effects=True, vmem_limit_bytes=52 * 1024 * 1024

time: 79.1 us -> 75.9 us (0.960)
  Pallas kernels: 78.2 us -> 74.9 us
    pallas_call x1, Pallas kernels: 76.7 us -> 73.5 us  [shards(): pl.pallas_call(functools.partial(kernel, n_blk, cells, lane_of), out_shap...]
where the time goes in v2:
time: 75.9 us; the launch traced here: 75.8 us
  Pallas kernels  74.9 us (99%)
  between operations  0.8 us (1%)
    pallas_call x1, Pallas kernels, shards(): pl.pallas_call(functools.partial(kernel, n_blk, cells, lane_of), out_shap...  73.5 us

profile of v2, /device:TPU:40, one launch (start us, length us, event | category | flops | bytes accessed | tf_op | source)
XLA Modules:
  0.0 75.8 jit_solution(8320126188100529729)
XLA Ops:
  0.6 73.5 %shard_map.112 = (f32[2,2,480,128]{3,2,1,0:T(8,128)S(1)}, f32[8,128]{1,0:T(8,128)S(1)}) custom-call(f32[8,2,480,128]{3,2,1,0:T(8,128)} %basis_hbm.1, s32[2,14]{1,0:T(2,128)} %nbr_block_hbm.1, s32[2,14]{1,0:T(2,128)} %nbr_type_hbm.1, s32[2]{0:T(128)} %nbr_count_hbm.1, s32[2,128]{1,0:T(2,128)} %sphere_type_hbm.1, s32[8,128]{1,0:T(8,128)} %constant.2.clone.table_hbm, ...), custom_call_target="tpu_custom_call" | custom-call | tf_op jit(solution)/shard_map/pallas_call | solution.py:581
  74.1 1.5 %shard_map.113 = (f32[2,2,480,128]{3,2,1,0:T(8,128)}, f32[9]{0:T(128)}, f32[10]{0:T(128)}) custom-call(f32[2,2,480,128]{3,2,1,0:T(8,128)S(1)} %get-tuple-element.5.new_in, f32[8,128]{1,0:T(8,128)S(1)} %get-tuple-element.6.hess), custom_call_target="tpu_custom_call" | custom-call | tf_op jit(solution)/shard_map/pallas_call | solution.py:640

commit v3 on v2

--- a/solution.py
+++ b/solution.py
@@ -209,14 +209,6 @@
         def _():
             halo(step, 1, r).wait_recv()
 
-    pl.semaphore_wait(
-        barrier, PLANE + 1 + far_left.astype(jnp.int32) + far_right.astype(jnp.int32)
-    )
-    own.wait()
-    for r in range(len(chunks)):
-        halo_start(0, r)
-    far_signal(0)
-
     @pl.when(jnp.logical_not(has_left))
     def _():
         wins[0, 0:n_loc] = jnp.zeros((n_loc, coef, sph), F32)
@@ -253,6 +245,14 @@
         return carry
 
     lax.fori_loop(0, kinds, split_coup, 0, unroll=4)
+
+    pl.semaphore_wait(
+        barrier, PLANE + 1 + far_left.astype(jnp.int32) + far_right.astype(jnp.int32)
+    )
+    own.wait()
+    for r in range(len(chunks)):
+        halo_start(0, r)
+    far_signal(0)
 
     def split_left(x, n):
         if n < LANES:
@@ -348,8 +348,6 @@
     def apply(step):
         last = len(chunks) - 1
         for r in range(len(chunks)):
-            if step == 0 and r > 0:
-                far_round(r - 1)
             halo_wait(step, r)
             mix(step, r)
             if r > 0:
@@ -375,6 +373,9 @@
                 acc[...] = jnp.where(here, part, acc[...])
             return carry
 
+        if step == 0:
+            for i in range(1, rounds - 1):
+                far_round(i)
         lax.fori_loop(0, s_kinds // 2, scatter, 0)
         for b in range(n_loc):
             image[b] = wins[step, n_loc + b] - acc[:, b * sph : (b + 1) * sph]
@@ -442,6 +443,9 @@
         ring_buf[step, z] = functools.reduce(
             jnp.add, [plane_buf[step, i] for i in range(PLANE)]
         )
+        if step == 0:
+            for i in range(max(1, rounds - 1), rounds):
+                far_round(i)
         order = sorted(range(1, n_ring), key=lambda d: -min(d, n_ring - d))
         for d in order:
             ring_copy(step, d).start()
@@ -487,6 +491,7 @@
         split_trans(r)
     tm_copy.wait()
     split_tmat()
+    far_round(0)
 
     apply(0)
     stack_copy.wait()

time: 75.9 us -> 74.1 us (0.976)
  Pallas kernels: 74.9 us -> 73.2 us
    pallas_call x1, Pallas kernels: 73.5 us -> 71.8 us  [shards(): pl.pallas_call(functools.partial(kernel, n_blk, cells, lane_of), out_shap...]
where the time goes in v3:
time: 74.1 us; the launch traced here: 74 us
  Pallas kernels  73.2 us (99%)
  between operations  0.8 us (1%)
    pallas_call x1, Pallas kernels, shards(): pl.pallas_call(functools.partial(kernel, n_blk, cells, lane_of), out_shap...  71.8 us

profile of v3, /device:TPU:40, one launch (start us, length us, event | category | flops | bytes accessed | tf_op | source)
XLA Modules:
  0.0 74.0 jit_solution(16300238723891236730)
XLA Ops:
  0.6 71.8 %shard_map.112 = (f32[2,2,480,128]{3,2,1,0:T(8,128)S(1)}, f32[8,128]{1,0:T(8,128)S(1)}) custom-call(f32[8,2,480,128]{3,2,1,0:T(8,128)} %basis_hbm.1, s32[2,14]{1,0:T(2,128)} %nbr_block_hbm.1, s32[2,14]{1,0:T(2,128)} %nbr_type_hbm.1, s32[2]{0:T(128)} %nbr_count_hbm.1, s32[2,128]{1,0:T(2,128)} %sphere_type_hbm.1, s32[8,128]{1,0:T(8,128)} %constant.2.clone.table_hbm, ...), custom_call_target="tpu_custom_call" | custom-call | tf_op jit(solution)/shard_map/pallas_call | solution.py:586
  72.4 1.5 %shard_map.113 = (f32[2,2,480,128]{3,2,1,0:T(8,128)}, f32[9]{0:T(128)}, f32[10]{0:T(128)}) custom-call(f32[2,2,480,128]{3,2,1,0:T(8,128)S(1)} %get-tuple-element.5.new_in, f32[8,128]{1,0:T(8,128)S(1)} %get-tuple-element.6.hess), custom_call_target="tpu_custom_call" | custom-call | tf_op jit(solution)/shard_map/pallas_call | solution.py:645
